TPU v7x, 32 devices: a whole 2x2x4 slice. The times are simulated.
32 devices in a mesh: grp: 2 (over y), col: 4 (over z), blk: 4 (over x, core).
Axes of the slice: x: 2, y: 2, z: 4, core: 2. Of those that a mesh axis runs over, the one named last changes fastest.
Arguments:
- boundary: bfloat16 [32, 192, 576], P(('grp', 'col'), 'blk'), parts along dimension 0, may hold values from -6 to 6
- row_tensor: bfloat16 [32, 6, 6, 6, 6], P(('grp', 'col')), parts along dimension 0, may hold values from -1.5 to 1.5
- left_proj: bfloat16 [32, 192, 576], P(('grp', 'col'), 'blk'), parts along dimension 0, may hold values from -0.75 to 0.75
- right_proj: bfloat16 [32, 192, 576], P(('grp', 'col'), 'blk'), parts along dimension 0, may hold values from -0.3125 to 0.3125
- leg_parity: int32 [32, 3, 6], P('grp'), parts along dimension 0, may hold values from 0 to 1
- bond_charges: int32 [32, 2], P('grp'), parts along dimension 0, may hold values from 32 to 96, as said below
Outputs:
- new_boundary: bfloat16 [32, 192, 576], P(('grp', 'col'), 'blk'), parts along dimension 0
There are 2 independent parts, one for each index of `grp`. A program takes and returns all parts, laid end to end along the dimension named above; each array names one. Nothing has to cross between parts.
Inputs may be any that keep to these rules, and one draw needn't show every extreme that they name: `bond_charges`: odd counts are 128 minus these, so neither block of a bond holds more than 96 live rows; some bond has an even count of 96 and some bond an odd count of 96. `leg_parity`: [c, 0] is the horizontal leg left of column c, [c, 1] the vertical leg between boundary and row, [c, 2] the outgoing vertical leg.
All inputs are finite; a program needn't handle non-finite values.
Results may differ from a plain program's by a relative error of at most 0.0057.
Values may be sent and summed in bfloat16 or wider, within the bound.
A program may use at most 64 MiB of HBM per device.

v0:
```python
import jax
import jax.numpy as jnp
from jax import lax
from jax.sharding import PartitionSpec as P

CHI = 128
BLOCK = 96
D = 6


def passed_along(x, axis, by):
    length = lax.axis_size(axis)
    return lax.ppermute(x, axis, [(i, (i + by) % length) for i in range(length)])


def live_rows(counts, parity, position):
    limit = jnp.where(parity == 0, counts, CHI - counts)
    return position < limit


def per_device(boundary, row_tensor, left_proj, right_proj, leg_parity, bond_charges):
    col_dev, sub_rows, merged = boundary.shape
    start_col = lax.axis_index("col") * col_dev
    charges_here = lax.dynamic_slice_in_dim(bond_charges, start_col, col_dev, 0)
    charges_next = lax.dynamic_slice_in_dim(jnp.roll(bond_charges, -1, 0), start_col, col_dev, 0)
    legs_here = lax.dynamic_slice_in_dim(leg_parity, start_col, col_dev, 0)
    legs_next = lax.dynamic_slice_in_dim(jnp.roll(leg_parity, -1, 0), start_col, col_dev, 0)
    in_here = charges_here[:, 0]
    out_here = charges_here[:, 1]
    in_next = charges_next[:, 0]
    out_next = charges_next[:, 1]
    left_leg = legs_here[:, 0]
    up_leg = legs_here[:, 1]
    down_leg = legs_here[:, 2]
    right_leg = legs_next[:, 0]
    inside = lax.iota(jnp.int32, BLOCK)
    row_start = lax.axis_index("blk") * sub_rows
    local_index = row_start + lax.iota(jnp.int32, sub_rows)
    local_parity = local_index // BLOCK
    local_position = local_index % BLOCK
    left_sel = (local_parity[None, :, None] + left_leg[:, None, :]) % 2
    left_mask = live_rows(out_here[:, None], local_parity[None, :], local_position[None, :])[
        :, :, None, None
    ] & live_rows(in_here[:, None, None, None], left_sel[..., None], inside[None, None, None, :])
    left_m = left_proj.reshape(col_dev, sub_rows, D, BLOCK) * left_mask.astype(jnp.bfloat16)
    left_dense = jnp.concatenate(
        [
            left_m * (left_sel == 0).astype(jnp.bfloat16)[..., None],
            left_m * (left_sel == 1).astype(jnp.bfloat16)[..., None],
        ],
        axis=3,
    )
    piece = lax.all_gather(boundary, "blk", axis=1, tiled=True)
    count_rows = piece.shape[1]
    row_index = lax.iota(jnp.int32, count_rows)
    row_parity = row_index // BLOCK
    row_position = row_index % BLOCK
    bound_sel = (row_parity[None, :, None] + up_leg[:, None, :]) % 2
    bound_mask = live_rows(in_here[:, None], row_parity[None, :], row_position[None, :])[
        :, :, None, None
    ] & live_rows(in_next[:, None, None, None], bound_sel[..., None], inside[None, None, None, :])
    piece_m = piece.reshape(col_dev, count_rows, D, BLOCK) * bound_mask.astype(jnp.bfloat16)
    absorbed = jnp.einsum(
        "cpla,caub->cplub", left_dense, piece_m, preferred_element_type=jnp.float32
    ).astype(jnp.bfloat16)
    row_keep = (
        left_leg[:, :, None, None, None]
        + up_leg[:, None, :, None, None]
        + down_leg[:, None, None, :, None]
        + right_leg[:, None, None, None, :]
    ) % 2 == 0
    row_sign = 1 - 2 * left_leg[:, :, None, None, None] * up_leg[:, None, :, None, None]
    row_m = row_tensor * jnp.where(row_keep, row_sign, 0).astype(jnp.bfloat16)
    mixed = jnp.einsum("cplub,cludr->cpdrb", absorbed, row_m, preferred_element_type=jnp.float32)
    block_par = (
        local_parity[None, :, None, None] + down_leg[:, None, :, None] + right_leg[:, None, None, :]
    ) % 2
    sign_flip = (1 - 2 * block_par * down_leg[:, None, :, None]).astype(jnp.float32)
    mixed = (mixed * sign_flip[..., None]).astype(jnp.bfloat16)
    mixed_dense = jnp.concatenate(
        [
            mixed * (block_par == 0).astype(jnp.bfloat16)[..., None],
            mixed * (block_par == 1).astype(jnp.bfloat16)[..., None],
        ],
        axis=4,
    )
    incoming = passed_along(right_proj[:1], "col", -1)
    right_next = jnp.concatenate([right_proj[1:], incoming], axis=0)
    piece = lax.all_gather(right_next, "blk", axis=1, tiled=True)
    count_rows = piece.shape[1]
    row_index = lax.iota(jnp.int32, count_rows)
    row_parity = row_index // BLOCK
    row_position = row_index % BLOCK
    right_sel = (row_parity[None, :, None] + right_leg[:, None, :]) % 2
    right_mask = live_rows(in_next[:, None], row_parity[None, :], row_position[None, :])[
        :, :, None, None
    ] & live_rows(out_next[:, None, None, None], right_sel[..., None], inside[None, None, None, :])
    piece_m = piece.reshape(col_dev, count_rows, D, BLOCK) * right_mask.astype(jnp.bfloat16)
    result = jnp.einsum(
        "cpdrb,cbre->cpde", mixed_dense, piece_m, preferred_element_type=jnp.float32
    )
    return result.astype(jnp.bfloat16).reshape(col_dev, sub_rows, merged)


def solution(mesh):
    in_specs = (
        P(("grp", "col"), "blk", None),
        P(("grp", "col"), None, None, None, None),
        P(("grp", "col"), "blk", None),
        P(("grp", "col"), "blk", None),
        P("grp", None, None),
        P("grp", None),
    )
    out_specs = P(("grp", "col"), "blk", None)
    return jax.shard_map(
        per_device, mesh=mesh, in_specs=in_specs, out_specs=out_specs, check_vma=False
    )
```

profile of v0, /device:TPU:0, one launch (start us, length us, event | category | flops | bytes accessed | tf_op | source)
XLA Modules:
  0.0 54.8 jit_solution(14372236034611323243)
XLA Ops:
  0.0 0.8 %slice.62 = bf16[1,48,576]{2,1,0:T(8,128)(2,1)S(1)} slice(bf16[4,48,576]{2,1,0:T(8,128)(2,1)} %param.9), slice={[0:1], [0:48], [0:576]} | slice | bytes 110592 | tf_op jit(solution)/shard_map/slice | solution.py:87
  0.8 5.1 %collective-permute-start = (bf16[1,48,576]{2,1,0:T(8,128)(2,1)S(1)}, bf16[1,48,576]{2,1,0:T(8,128)(2,1)S(1)}, u32[]{:S(2)}, u32[]{:S(2)}) collective-permute-start(bf16[1,48,576]{2,1,0:T(8,128)(2,1)S(1)} %slice.62), channel_id=1, source_target_pairs={{0,12},{4,0},{8,4},{12,8},{1,13},{5,1},{9,5},{13,9},{2,14},{6,2},{... | collective-permute-start | bytes 165896 | tf_op jit(solution)/shard_map/ppermute | solution.py:13
  5.9 0.7 %slice.57 = s32[15,2]{0,1:T(2,128)S(1)} slice(s32[16,2]{0,1:T(2,128)} %param.11), slice={[1:16], [0:2]} | slice | bytes 240 | tf_op jit(solution)/shard_map/jit(_roll_static)/slice | solution.py:25
  6.7 0.8 %pad_add_fusion = s32[16,2]{0,1:T(2,128)S(1)} fusion(s32[1,2]{0,1:T(2,128)} %bitcast.75, s32[15,2]{0,1:T(2,128)S(1)} %slice.57), kind=kLoop, calls=%fused_computation.102 | loop fusion | flops 32 | bytes 256 | tf_op jit(solution)/shard_map/jit(_roll_static)/concatenate | solution.py:25
  7.4 0.8 %constant_dynamic-slice_fusion.2 = (s32[4,2]{0,1:T(2,128)S(1)}, s32[4,2]{0,1:T(2,128)S(1)}) fusion(s32[16,2]{0,1:T(2,128)S(1)} %pad_add_fusion, s32[]{:T(128)S(6)} %select_n.177, s32[16,2]{0,1:T(2,128)} %param.11), kind=kLoop, calls=%fused_computation.97 | loop fusion | bytes 132 | tf_op jit(solution)/shard_map/dynamic_slice | solution.py:25
  8.3 0.8 %slice.51 = s32[15,3,6]{0,2,1:T(8,128)S(1)} slice(s32[16,3,6]{0,2,1:T(8,128)} %param.10), slice={[1:16], [0:3], [0:6]} | slice | bytes 2160 | tf_op jit(solution)/shard_map/jit(_roll_static)/slice | solution.py:27
  9.1 0.8 %constant_dynamic-slice_fusion.1 = (s32[4,1,6]{0,2,1:T(8,128)S(1)}, s32[4,1,6]{0,2,1:T(8,128)S(1)}, s32[4,1,6]{0,2,1:T(8,128)S(1)}, s32[4,1,6]{0,2,1:T(8,128)S(1)}) fusion(s32[16,3,6]{0,2,1:T(8,128)} %param.10, s32[]{:T(128)S(6)} %select_n.177, s32[]{:T(128)S(6)} %add.320, s32[]{:T(128)S(6)} %add.321, s32[1,3,6]{0,2,1:T(8,128)} %bitcast.63, ...), kind=kLoop, calls=%fused_computation.96 | loop fusion | flops 24 | bytes 1836 | tf_op jit(solution)/shard_map/slice | solution.py:32
  9.9 0.1 copy.38
  10.0 0.1 copy.42
  10.1 0.1 copy.39
  10.3 1.3 %reshape.409 = bf16[4,48,6,96]{3,2,1,0:T(8,128)(2,1)S(1)} reshape(bf16[4,48,576]{2,1,0:T(8,128)(2,1)} %param.8) | data formatting | bytes 442368 | tf_op jit(solution)/shard_map/reshape | solution.py:45
  11.6 0.1 copy.44
  11.7 0.1 copy.40
  11.8 1.0 %copy.47 = bf16[4,48,576]{2,0,1:T(4,128)(2,1)S(1)} copy(bf16[4,48,576]{2,1,0:T(8,128)(2,1)} %param.6) | data formatting | bytes 442368 | tf_op args[0]
  12.8 9.8 %all_gather.6 = bf16[4,192,576]{2,0,1:T(4,128)(2,1)S(1)} all-gather(bf16[4,48,576]{2,0,1:T(4,128)(2,1)S(1)} %copy.47), channel_id=1, replica_groups=mesh['grp'=2,'col'=4,'blk'=4] {'blk'}, dimensions={1}, use_global_device_ids=true | all-gather | bytes 1105920 | tf_op jit(solution)/shard_map/all_gather | solution.py:53
  22.6 1.3 %copy.48 = bf16[4,192,576]{1,2,0:T(8,128)(2,1)S(1)} copy(bf16[4,192,576]{2,0,1:T(4,128)(2,1)S(1)} %all_gather.6) | data formatting | bytes 1769472 | tf_op jit(solution)/shard_map/all_gather | solution.py:53
  23.9 0.1 copy.45
  24.1 0.1 copy.43
  24.3 0.4 compare_convert_fusion.1
  24.7 0.4 subtract_convert_fusion
  25.1 0.7 %fusion.36 = bf16[4,6,6,6,6,1]{4,0,3,2,1,5:T(4,128)(2,1)S(1)} fusion(bf16[4,6,6,6,6]{4,0,3,2,1:T(4,128)(2,1)S(1)} %copy-done, s32[4,6,6]{0,2,1:T(8,128)S(1)} %get-tuple-element.15, s32[4,6]{1,0:T(4,128)S(1)} %bitcast.66, s32[4,6,6,6]{0,3,2,1:T(8,128)S(1)} %broadcast_add_fusion), kind=kLoop, calls=%fused_computation.52 | loop fusion | flops 98496 | bytes 24864 | tf_op jit(solution)/shard_map/mul | solution.py:73
  25.9 0.1 fusion.41
  26.1 0.6 %broadcast_multiply_fusion.3 = (bf16[4,48,6,96]{3,1,2,0:T(8,128)(2,1)S(1)}, bf16[4,48,6,96]{3,1,2,0:T(8,128)(2,1)S(1)}) fusion(bf16[4,48,6]{1,2,0:T(8,128)(2,1)S(1)} %get-tuple-element.16, bf16[4,48,6,96]{3,2,1,0:T(8,128)(2,1)S(1)} %reshape.409, s32[4,48,6]{1,2,0:T(8,128)S(1)} %get-tuple-element.31, pred[4,48]{1,0:T(4,128)(4,1)S(1)} %select_compare_fusion.2, ...), kind=kLoop, calls=%fused_computation.54 | loop fusion | flops 1105920 | bytes 672960 | tf_op jit(solution)/shard_map/mul | solution.py:48
  26.7 1.0 %convert_bitcast_fusion = bf16[4,48,6,6,96,1]{4,1,3,2,0,5:T(8,128)(2,1)S(1)} fusion(bf16[4,192,6,96]{1,3,2,0:T(8,128)(2,1)S(1)} %bitcast.61, s32[4,192,6]{1,2,0:T(8,128)S(1)} %get-tuple-element.24, pred[4,192]{1,0:T(4,128)(4,1)S(1)} %get-tuple-element.19, bf16[4,48,6,96]{3,1,2,0:T(8,128)(2,1)S(1)} %get-tuple-element.8, ...), kind=kOutput, calls=%fused_computation.13 | convolution fusion | flops 257679360 | bytes 2673408 | tf_op jit(solution)/shard_map/cpla,caub->cplub/dot_general | solution.py:63
  27.7 6.6 %broadcast_multiply_fusion.1 = (bf16[4,48,6,6,96]{4,3,1,2,0:T(8,128)(2,1)S(1)}, bf16[4,48,6,6,96]{4,3,1,2,0:T(8,128)(2,1)S(1)}) fusion(bf16[4,48,6,6]{3,1,2,0:T(8,128)(2,1)S(1)} %get-tuple-element.9, bf16[4,48,6,6]{3,1,2,0:T(8,128)(2,1)S(1)} %get-tuple-element.10, f32[4,48,6,6]{3,1,2,0:T(8,128)S(1)} %subtract_convert_fusion, ...), kind=kOutput, calls=%fused_computation.20 | convolution fusion | flops 50429952 | bytes 4046976 | tf_op jit(solution)/shard_map/cplub,cludr->cpdrb/dot_general | solution.py:74
  34.3 4.5 %pad_maximum_fusion = bf16[4,48,6,6,192]{4,3,1,2,0:T(8,128)(2,1)} fusion(bf16[4,48,6,6,96]{4,3,1,2,0:T(8,128)(2,1)S(1)} %get-tuple-element.6, bf16[4,48,6,6,96]{4,3,1,2,0:T(8,128)(2,1)S(1)} %get-tuple-element.5), kind=kLoop, calls=%fused_computation | loop fusion | flops 5308416 | bytes 5308416 | tf_op jit(solution)/shard_map/concatenate | solution.py:80
  38.9 0.1 copy.52
  39.0 9.8 %all_gather.7 = bf16[4,192,576]{2,0,1:T(4,128)(2,1)S(1)} all-gather(bf16[4,48,576]{2,0,1:T(4,128)(2,1)S(1)} %copy.52), channel_id=1, replica_groups=mesh['grp'=2,'col'=4,'blk'=4] {'blk'}, dimensions={1}, use_global_device_ids=true | all-gather | bytes 1105920 | tf_op jit(solution)/shard_map/all_gather | solution.py:89
  48.7 1.3 %copy.53 = bf16[4,192,576]{1,2,0:T(8,128)(2,1)S(1)} copy(bf16[4,192,576]{2,0,1:T(4,128)(2,1)S(1)} %all_gather.7) | data formatting | bytes 1769472 | tf_op jit(solution)/shard_map/all_gather | solution.py:89
  50.0 3.7 %fusion.14 = bf16[4,48,6,96]{3,1,2,0:T(8,128)(2,1)S(1)} fusion(bf16[4,48,6,6,192]{4,3,1,2,0:T(8,128)(2,1)} %pad_maximum_fusion, bf16[4,192,6,96]{1,3,2,0:T(8,128)(2,1)S(1)} %bitcast.62, s32[4,192,6]{1,2,0:T(8,128)S(1)} %get-tuple-element.23, pred[4,192]{1,0:T(4,128)(4,1)S(1)} %get-tuple-element.18), kind=kOutput, calls=%fused_computation.15 | convolution fusion | flops 256241664 | bytes 3779328 | tf_op jit(solution)/shard_map/cpdrb,cbre->cpde/dot_general | solution.py:99
  53.7 0.1 copy.56
  53.8 1.0 %reshape.412 = bf16[4,48,576]{2,1,0:T(8,128)(2,1)} reshape(bf16[4,48,6,96]{3,2,1,0:T(8,128)(2,1)S(1)} %copy.56) | data formatting | bytes 442368 | tf_op jit(solution)/shard_map/reshape | solution.py:102
  (23 shorter events, 0.6 us)
Async XLA Ops:
  0.8 38.0 %collective-permute-start = (bf16[1,48,576]{2,1,0:T(8,128)(2,1)S(1)}, bf16[1,48,576]{2,1,0:T(8,128)(2,1)S(1)}, u32[]{:S(2)}, u32[]{:S(2)}) collective-permute-start(bf16[1,48,576]{2,1,0:T(8,128)(2,1)S(1)} %slice.62), channel_id=1, source_target_pairs={{0,12},{4,0},{8,4},{12,8},{1,13},{5,1},{9,5},{13,9},{2,14},{6,2},{... | collective-permute-start | bytes 165896 | tf_op jit(solution)/shard_map/ppermute | solution.py:13
  12.8 12.3 %copy-start = (bf16[4,6,6,6,6]{4,0,3,2,1:T(4,128)(2,1)S(1)}, bf16[4,6,6,6,6]{4,0,3,2,1:T(4,128)(2,1)}, u32[]{:S(2)}) copy-start(bf16[4,6,6,6,6]{4,0,3,2,1:T(4,128)(2,1)} %param.7) | copy-start | bytes 31108
  34.3 4.5 %slice-start = ((bf16[4,48,576]{2,1,0:T(8,128)(2,1)}), bf16[3,48,576]{2,1,0:T(8,128)(2,1)S(1)}, s32[]{:S(2)}) async-start(bf16[4,48,576]{2,1,0:T(8,128)(2,1)} %param.9), calls=%async_computation | async-start | bytes 368640 | tf_op jit(solution)/shard_map/slice | solution.py:88
where the time goes:
time: 55.2 us; the launch traced here: 54.8 us
  blocking collectives  19.6 us (36%)
  matrix products  11.3 us (20%)
  local copies, waits for them, and re-layouts  9.95 us (18%)
  other arithmetic  8.7 us (16%)
  starting transfers between devices  5.08 us (9%)
    all_gather x1, blocking collectives, per_device(): piece = lax.all_gather(boundary, 'blk', axis=1, tiled=True)  9.8 us
    all_gather x1, blocking collectives, per_device(): piece = lax.all_gather(right_next, 'blk', axis=1, tiled=True)  9.78 us
    dot_general x1, matrix products, per_device(): jnp.einsum('cplub,cludr->cpdrb', absorbed, row_m, preferred_element_type=...  6.63 us
    ppermute x1, starting transfers between devices, passed_along(): lax.ppermute(x, axis, [(i, (i + by) % length) for i in range(length)])  5.08 us
    concatenate x1, other arithmetic, per_device(): jnp.concatenate([mixed * (block_par == 0).astype(jnp.bfloat16)[..., None]...  4.46 us
    dot_general x1, matrix products, per_device(): jnp.einsum('cpdrb,cbre->cpde', mixed_dense, piece_m, preferred_element_ty...  3.67 us
    reshape x1, local copies, waits for them, and re-layouts, per_device(): left_proj.reshape(col_dev, sub_rows, D, BLOCK)  1.31 us
    all_gather x1, local copies, waits for them, and re-layouts, per_device(): piece = lax.all_gather(boundary, 'blk', axis=1, tiled=True)  1.27 us
  transfers between devices with their start and end apart: 1, of which 0 were waited for; matrix products, arithmetic and copies ran while one was open for 42% of the time, Pallas kernels for 0%

commit v1 on v0

--- a/solution.py
+++ b/solution.py
@@ -86,7 +86,12 @@
     )
     incoming = passed_along(right_proj[:1], "col", -1)
     right_next = jnp.concatenate([right_proj[1:], incoming], axis=0)
-    piece = lax.all_gather(right_next, "blk", axis=1, tiled=True)
+    ring = [right_next]
+    for hop in range(3):
+        ring.append(lax.ppermute(ring[-1], "blk", [(dev, (dev + 1) % 4) for dev in range(4)]))
+    piece = jnp.roll(
+        jnp.concatenate(ring[::-1], axis=1), (lax.axis_index("blk") + 1) * ring[0].shape[1], axis=1
+    )
     count_rows = piece.shape[1]
     row_index = lax.iota(jnp.int32, count_rows)
     row_parity = row_index // BLOCK

time: 55.2 us -> 62.8 us (1.14)
  blocking collectives: 19.6 us -> 9.67 us
  local copies, waits for them, and re-layouts: 9.95 us -> 18.1 us
  waiting for transfers between devices: 0.01 us -> 4.86 us
  other arithmetic: 8.7 us -> 10.3 us
  matrix products: 11.3 us -> 12.8 us
  starting transfers between devices: 5.08 us -> 6.4 us
    all_gather x1 -> x0, blocking collectives: 9.78 us -> none  [per_device(): piece = lax.all_gather(right_next, 'blk', axis=1, tiled=True)]
    concatenate x0 -> x1, local copies, waits for them, and re-layouts: none -> 6.45 us  [per_device(): jnp.roll(jnp.concatenate(ring[::-1], axis=1), (lax.axis_index('blk') + 1)...]
    ppermute x0 -> x3, waiting for transfers between devices: none -> 4.86 us  [per_device(): lax.ppermute(ring[-1], 'blk', [(dev, (dev + 1) % 4) for dev in range(4)])]
    dynamic_slice x0 -> x1, local copies, waits for them, and re-layouts: none -> 1.82 us  [per_device(): jnp.roll(jnp.concatenate(ring[::-1], axis=1), (lax.axis_index('blk') + 1)...]
    concatenate x1, other arithmetic: 4.46 us -> 6.09 us  [per_device(): jnp.concatenate([mixed * (block_par == 0).astype(jnp.bfloat16)[..., None]...]
    dot_general x1, matrix products: 6.63 us -> 8.11 us  [per_device(): jnp.einsum('cplub,cludr->cpdrb', absorbed, row_m, preferred_element_type=...]
    ppermute x0 -> x3, starting transfers between devices: none -> 1.32 us  [per_device(): lax.ppermute(ring[-1], 'blk', [(dev, (dev + 1) % 4) for dev in range(4)])]
    all_gather x1 -> x0, local copies, waits for them, and re-layouts: 1.27 us -> none  [per_device(): piece = lax.all_gather(right_next, 'blk', axis=1, tiled=True)]
  transfers between devices with their start and end apart: 1 -> 4, of which waited for: 0 -> 1; matrix products, arithmetic and copies ran while one was open for 42% -> 43% of each run, Pallas kernels for 0% -> 0%
where the time goes in v1:
time: 62.8 us; the launch traced here: 62.3 us
  local copies, waits for them, and re-layouts  18.1 us (29%)
  matrix products  12.8 us (20%)
  other arithmetic  10.3 us (16%)
  blocking collectives  9.67 us (15%)
  starting transfers between devices  6.4 us (10%)
  waiting for transfers between devices  4.86 us (8%)
    all_gather x1, blocking collectives, per_device(): piece = lax.all_gather(boundary, 'blk', axis=1, tiled=True)  9.67 us
    dot_general x1, matrix products, per_device(): jnp.einsum('cplub,cludr->cpdrb', absorbed, row_m, preferred_element_type=...  8.11 us
    concatenate x1, local copies, waits for them, and re-layouts, per_device(): jnp.roll(jnp.concatenate(ring[::-1], axis=1), (lax.axis_index('blk') + 1)...  6.45 us
    concatenate x1, other arithmetic, per_device(): jnp.concatenate([mixed * (block_par == 0).astype(jnp.bfloat16)[..., None]...  6.09 us
    ppermute x1, starting transfers between devices, passed_along(): lax.ppermute(x, axis, [(i, (i + by) % length) for i in range(length)])  5.08 us
    ppermute x3, waiting for transfers between devices, per_device(): lax.ppermute(ring[-1], 'blk', [(dev, (dev + 1) % 4) for dev in range(4)])  4.86 us
    dot_general x1, matrix products, per_device(): jnp.einsum('cpdrb,cbre->cpde', mixed_dense, piece_m, preferred_element_ty...  3.67 us
    dynamic_slice x1, local copies, waits for them, and re-layouts, per_device(): jnp.roll(jnp.concatenate(ring[::-1], axis=1), (lax.axis_index('blk') + 1)...  1.82 us
  transfers between devices with their start and end apart: 4, of which 1 were waited for; matrix products, arithmetic and copies ran while one was open for 43% of the time, Pallas kernels for 0%

profile of v1, /device:TPU:0, one launch (start us, length us, event | category | flops | bytes accessed | tf_op | source)
XLA Modules:
  0.0 62.3 jit_solution(6424357752129689720)
XLA Ops:
  0.0 0.8 %slice.62 = bf16[1,48,576]{2,1,0:T(8,128)(2,1)S(1)} slice(bf16[4,48,576]{2,1,0:T(8,128)(2,1)} %param.9), slice={[0:1], [0:48], [0:576]} | slice | bytes 110592 | tf_op jit(solution)/shard_map/slice | solution.py:87
  0.8 5.1 %collective-permute-start = (bf16[1,48,576]{2,1,0:T(8,128)(2,1)S(1)}, bf16[1,48,576]{2,1,0:T(8,128)(2,1)S(1)}, u32[]{:S(2)}, u32[]{:S(2)}) collective-permute-start(bf16[1,48,576]{2,1,0:T(8,128)(2,1)S(1)} %slice.62), channel_id=1, source_target_pairs={{0,12},{4,0},{8,4},{12,8},{1,13},{5,1},{9,5},{13,9},{2,14},{6,2},{... | collective-permute-start | bytes 165896 | tf_op jit(solution)/shard_map/ppermute | solution.py:13
  5.9 0.7 %slice.57 = s32[15,2]{0,1:T(2,128)S(1)} slice(s32[16,2]{0,1:T(2,128)} %param.11), slice={[1:16], [0:2]} | slice | bytes 240 | tf_op jit(solution)/shard_map/jit(_roll_static)/slice | solution.py:25
  6.7 0.8 %pad_add_fusion = s32[16,2]{0,1:T(2,128)S(1)} fusion(s32[1,2]{0,1:T(2,128)} %bitcast.75, s32[15,2]{0,1:T(2,128)S(1)} %slice.57), kind=kLoop, calls=%fused_computation.103 | loop fusion | flops 32 | bytes 256 | tf_op jit(solution)/shard_map/jit(_roll_static)/concatenate | solution.py:25
  7.4 0.8 %constant_dynamic-slice_fusion.3 = (s32[4,2]{0,1:T(2,128)S(1)}, s32[4,2]{0,1:T(2,128)S(1)}) fusion(s32[16,2]{0,1:T(2,128)S(1)} %pad_add_fusion, s32[]{:T(128)S(6)} %select_n.189, s32[16,2]{0,1:T(2,128)} %param.11), kind=kLoop, calls=%fused_computation.94 | loop fusion | bytes 132 | tf_op jit(solution)/shard_map/dynamic_slice | solution.py:25
  8.3 0.8 %slice.51 = s32[15,3,6]{0,2,1:T(8,128)S(1)} slice(s32[16,3,6]{0,2,1:T(8,128)} %param.10), slice={[1:16], [0:3], [0:6]} | slice | bytes 2160 | tf_op jit(solution)/shard_map/jit(_roll_static)/slice | solution.py:27
  9.1 0.8 %constant_dynamic-slice_fusion.1 = (s32[4,1,6]{0,2,1:T(8,128)S(1)}, s32[4,1,6]{0,2,1:T(8,128)S(1)}, s32[4,1,6]{0,2,1:T(8,128)S(1)}, s32[4,1,6]{0,2,1:T(8,128)S(1)}) fusion(s32[16,3,6]{0,2,1:T(8,128)} %param.10, s32[]{:T(128)S(6)} %select_n.189, s32[]{:T(128)S(6)} %add.336, s32[]{:T(128)S(6)} %add.337, s32[1,3,6]{0,2,1:T(8,128)} %bitcast.63, ...), kind=kLoop, calls=%fused_computation.92 | loop fusion | flops 24 | bytes 1836 | tf_op jit(solution)/shard_map/slice | solution.py:32
  10.3 1.3 %reshape.409 = bf16[4,48,6,96]{3,2,1,0:T(8,128)(2,1)S(1)} reshape(bf16[4,48,576]{2,1,0:T(8,128)(2,1)} %param.8) | data formatting | bytes 442368 | tf_op jit(solution)/shard_map/reshape | solution.py:45
  11.6 0.1 copy.43
  11.8 1.0 %copy.46 = bf16[4,48,576]{2,0,1:T(4,128)(2,1)S(1)} copy(bf16[4,48,576]{2,1,0:T(8,128)(2,1)} %param.6) | data formatting | bytes 442368 | tf_op args[0]
  12.9 9.7 %all_gather.3 = bf16[4,192,576]{2,0,1:T(4,128)(2,1)S(1)} all-gather(bf16[4,48,576]{2,0,1:T(4,128)(2,1)S(1)} %copy.46), channel_id=1, replica_groups=mesh['grp'=2,'col'=4,'blk'=4] {'blk'}, dimensions={1}, use_global_device_ids=true | all-gather | bytes 1105920 | tf_op jit(solution)/shard_map/all_gather | solution.py:53
  22.5 1.3 %copy.47 = bf16[4,192,576]{1,2,0:T(8,128)(2,1)S(1)} copy(bf16[4,192,576]{2,0,1:T(4,128)(2,1)S(1)} %all_gather.3) | data formatting | bytes 1769472 | tf_op jit(solution)/shard_map/all_gather | solution.py:53
  24.3 0.7 %fusion.36 = bf16[4,6,6,6,6,1]{4,0,3,2,1,5:T(4,128)(2,1)S(1)} fusion(bf16[4,6,6,6,6]{4,0,3,2,1:T(4,128)(2,1)S(1)} %copy-done, s32[4,6,6]{0,2,1:T(8,128)S(1)} %get-tuple-element.15, s32[4,6]{1,0:T(4,128)S(1)} %bitcast.64, s32[4,6,6,6]{0,3,2,1:T(8,128)S(1)} %broadcast_add_fusion), kind=kLoop, calls=%fused_computation.52 | loop fusion | flops 98496 | bytes 24864 | tf_op jit(solution)/shard_map/mul | solution.py:73
  25.0 0.1 fusion.41
  25.1 0.6 %broadcast_multiply_fusion.3 = (bf16[4,48,6,96]{3,1,2,0:T(8,128)(2,1)S(1)}, bf16[4,48,6,96]{3,1,2,0:T(8,128)(2,1)S(1)}) fusion(bf16[4,48,6]{1,2,0:T(8,128)(2,1)S(1)} %get-tuple-element.16, bf16[4,48,6,96]{3,2,1,0:T(8,128)(2,1)S(1)} %reshape.409, s32[4,48,6]{1,2,0:T(8,128)S(1)} %get-tuple-element.31, pred[4,48]{1,0:T(4,128)(4,1)S(1)} %select_compare_fusion.2, ...), kind=kLoop, calls=%fused_computation.54 | loop fusion | flops 1105920 | bytes 672960 | tf_op jit(solution)/shard_map/mul | solution.py:48
  25.8 1.0 %convert_bitcast_fusion = bf16[4,48,6,6,96,1]{4,1,3,2,0,5:T(8,128)(2,1)S(1)} fusion(bf16[4,192,6,96]{1,3,2,0:T(8,128)(2,1)S(1)} %bitcast.62, s32[4,192,6]{1,2,0:T(8,128)S(1)} %get-tuple-element.24, pred[4,192]{1,0:T(4,128)(4,1)S(1)} %get-tuple-element.19, bf16[4,48,6,96]{3,1,2,0:T(8,128)(2,1)S(1)} %get-tuple-element.8, ...), kind=kOutput, calls=%fused_computation.13 | convolution fusion | flops 257679360 | bytes 2673408 | tf_op jit(solution)/shard_map/cpla,caub->cplub/dot_general | solution.py:63
  26.8 0.4 subtract_convert_fusion
  27.2 0.4 collective-permute-start.1
  27.6 0.4 compare_convert_fusion.1
  28.1 4.9 %collective-permute-done.1 = bf16[4,48,576]{2,1,0:T(8,128)(2,1)S(1)} collective-permute-done((bf16[4,48,576]{2,1,0:T(8,128)(2,1)S(1)}, bf16[4,48,576]{2,1,0:T(8,128)(2,1)S(1)}, u32[]{:S(2)}, u32[]{:S(2)}) %collective-permute-start.1) | collective-permute-done | bytes 221216 | tf_op jit(solution)/shard_map/ppermute | solution.py:91
  32.9 8.1 %broadcast_multiply_fusion.1 = (bf16[4,48,6,6,96]{4,3,1,2,0:T(8,128)(2,1)S(1)}, bf16[4,48,6,6,96]{4,3,1,2,0:T(8,128)(2,1)}) fusion(bf16[4,48,6,6]{3,1,2,0:T(8,128)(2,1)S(1)} %get-tuple-element.9, bf16[4,48,6,6]{3,1,2,0:T(8,128)(2,1)S(1)} %get-tuple-element.10, f32[4,48,6,6]{3,1,2,0:T(8,128)S(1)} %subtract_convert_fusion, ...), kind=kOutput, calls=%fused_computation.20 | convolution fusion | flops 50429952 | bytes 4046976 | tf_op jit(solution)/shard_map/cplub,cludr->cpdrb/dot_general | solution.py:74
  41.0 0.9 %collective-permute-start.3 = (bf16[4,48,576]{2,1,0:T(8,128)(2,1)S(1)}, bf16[4,48,576]{2,1,0:T(8,128)(2,1)S(1)}, u32[]{:S(2)}, u32[]{:S(2)}) collective-permute-start(bf16[4,48,576]{2,1,0:T(8,128)(2,1)S(1)} %collective-permute-done.2), channel_id=1, source_target_pairs={{0,1},{1,2},{2,3},{3,0},{4,5},{5,6},{6,7},{7,4},{8,9},{9,10},{10,1... | collective-permute-start | bytes 663560 | tf_op jit(solution)/shard_map/ppermute | solution.py:91
  41.9 6.1 %pad_maximum_fusion = bf16[4,48,6,6,192]{4,3,1,2,0:T(8,128)(2,1)} fusion(bf16[4,48,6,6,96]{4,3,1,2,0:T(8,128)(2,1)} %get-tuple-element.6, bf16[4,48,6,6,96]{4,3,1,2,0:T(8,128)(2,1)S(1)} %get-tuple-element.5), kind=kLoop, calls=%fused_computation | loop fusion | flops 5308416 | bytes 5308416 | tf_op jit(solution)/shard_map/concatenate | solution.py:80
  48.0 0.3 copy.54
  48.3 0.3 copy.53
  48.7 0.3 copy.52
  49.0 0.3 copy.51
  49.3 6.5 %concatenate.28 = bf16[4,384,576]{1,2,0:T(8,128)(2,1)} concatenate(bf16[4,48,576]{1,2,0:T(8,128)(2,1)S(1)} %copy.51, bf16[4,48,576]{1,2,0:T(8,128)(2,1)S(1)} %copy.52, bf16[4,48,576]{1,2,0:T(8,128)(2,1)S(1)} %copy.53, bf16[4,48,576]{1,2,0:T(8,128)(2,1)S(1)} %copy.54, bf16[4,48,576]{1,2,0:T(8,128)(2,1)S(1)} %copy.51, bf16[4,48,576]{1,2,0:T(8,128)(2,1)S(1)} %copy.52, ...), dimensions={1} | concatenate | bytes 3538944 | tf_op jit(solution)/shard_map/jit(_roll_dynamic)/concatenate | solution.py:92
  55.7 1.8 %constant_dynamic-slice_fusion.2 = bf16[4,192,576]{1,2,0:T(8,128)(2,1)S(1)} fusion(bf16[4,384,576]{1,2,0:T(8,128)(2,1)} %concatenate.28, s32[]{:T(128)S(6)} %select_n.207), kind=kLoop, calls=%fused_computation.93 | loop fusion | bytes 1769476 | tf_op jit(solution)/shard_map/jit(_roll_dynamic)/dynamic_slice | solution.py:92
  57.5 3.7 %fusion.14 = bf16[4,48,6,96]{3,1,2,0:T(8,128)(2,1)S(1)} fusion(bf16[4,48,6,6,192]{4,3,1,2,0:T(8,128)(2,1)} %pad_maximum_fusion, bf16[4,192,6,96]{1,3,2,0:T(8,128)(2,1)S(1)} %bitcast.61, s32[4,192,6]{1,2,0:T(8,128)S(1)} %get-tuple-element.23, pred[4,192]{1,0:T(4,128)(4,1)S(1)} %get-tuple-element.18), kind=kOutput, calls=%fused_computation.15 | convolution fusion | flops 256241664 | bytes 3779328 | tf_op jit(solution)/shard_map/cpdrb,cbre->cpde/dot_general | solution.py:104
  61.2 0.1 copy.61
  61.3 1.0 %reshape.412 = bf16[4,48,576]{2,1,0:T(8,128)(2,1)} reshape(bf16[4,48,6,96]{3,2,1,0:T(8,128)(2,1)S(1)} %copy.61) | data formatting | bytes 442368 | tf_op jit(solution)/shard_map/reshape | solution.py:107
  (32 shorter events, 1.1 us)
Async XLA Ops:
  0.8 26.3 %collective-permute-start = (bf16[1,48,576]{2,1,0:T(8,128)(2,1)S(1)}, bf16[1,48,576]{2,1,0:T(8,128)(2,1)S(1)}, u32[]{:S(2)}, u32[]{:S(2)}) collective-permute-start(bf16[1,48,576]{2,1,0:T(8,128)(2,1)S(1)} %slice.62), channel_id=1, source_target_pairs={{0,12},{4,0},{8,4},{12,8},{1,13},{5,1},{9,5},{13,9},{2,14},{6,2},{... | collective-permute-start | bytes 165896 | tf_op jit(solution)/shard_map/ppermute | solution.py:13
  10.3 14.0 %copy-start = (bf16[4,6,6,6,6]{4,0,3,2,1:T(4,128)(2,1)S(1)}, bf16[4,6,6,6,6]{4,0,3,2,1:T(4,128)(2,1)}, u32[]{:S(2)}) copy-start(bf16[4,6,6,6,6]{4,0,3,2,1:T(4,128)(2,1)} %param.7) | copy-start | bytes 31108
  25.8 1.4 %slice-start = ((bf16[4,48,576]{2,1,0:T(8,128)(2,1)}), bf16[3,48,576]{2,1,0:T(8,128)(2,1)S(1)}, s32[]{:S(2)}) async-start(bf16[4,48,576]{2,1,0:T(8,128)(2,1)} %param.9), calls=%async_computation | async-start | bytes 368640 | tf_op jit(solution)/shard_map/slice | solution.py:88
  27.2 5.7 %collective-permute-start.1 = (bf16[4,48,576]{2,1,0:T(8,128)(2,1)S(1)}, bf16[4,48,576]{2,1,0:T(8,128)(2,1)S(1)}, u32[]{:S(2)}, u32[]{:S(2)}) collective-permute-start(bf16[4,48,576]{2,1,0:T(8,128)(2,1)S(1)} %pad_maximum_fusion.1), channel_id=1, source_target_pairs={{0,1},{1,2},{2,3},{3,0},{4,5},{5,6},{6,7},{7,4},{8,9},{9,10},{10,1... | collective-permute-start | bytes 663560 | tf_op jit(solution)/shard_map/ppermute | solution.py:91
  32.9 8.1 %collective-permute-start.2 = (bf16[4,48,576]{2,1,0:T(8,128)(2,1)S(1)}, bf16[4,48,576]{2,1,0:T(8,128)(2,1)S(1)}, u32[]{:S(2)}, u32[]{:S(2)}) collective-permute-start(bf16[4,48,576]{2,1,0:T(8,128)(2,1)S(1)} %collective-permute-done.1), channel_id=1, source_target_pairs={{0,1},{1,2},{2,3},{3,0},{4,5},{5,6},{6,7},{7,4},{8,9},{9,10},{10,1... | collective-permute-start | bytes 663560 | tf_op jit(solution)/shard_map/ppermute | solution.py:91
  41.0 7.9 %collective-permute-start.3 = (bf16[4,48,576]{2,1,0:T(8,128)(2,1)S(1)}, bf16[4,48,576]{2,1,0:T(8,128)(2,1)S(1)}, u32[]{:S(2)}, u32[]{:S(2)}) collective-permute-start(bf16[4,48,576]{2,1,0:T(8,128)(2,1)S(1)} %collective-permute-done.2), channel_id=1, source_target_pairs={{0,1},{1,2},{2,3},{3,0},{4,5},{5,6},{6,7},{7,4},{8,9},{9,10},{10,1... | collective-permute-start | bytes 663560 | tf_op jit(solution)/shard_map/ppermute | solution.py:91
